TPU v7x, 32 devices: a whole 2x2x4 slice. The times are simulated.
32 devices in a mesh: rep: 1, r: 4 (over z), s: 8 (over x, y, core).
Axes of the slice: x: 2, y: 2, z: 4, core: 2. Of those that a mesh axis runs over, the one named last changes fastest.
Arguments:
- x: bfloat16 [32, 4096, 640], P(('rep', 'r', 's'))
- dy: bfloat16 [32, 4096, 640], P(('rep', 'r', 's'))
- w_gate: bfloat16 [2, 640, 2048], P(None, 's')
- w_up: bfloat16 [2, 640, 2048], P(None, 's')
- w_down: bfloat16 [2, 2048, 640], P(None, 's')
Outputs:
- output 1: bfloat16 [32, 4096, 640], P(('rep', 'r', 's'))
- output 2: bfloat16 [2, 640, 2048], P('rep', 's')
- output 3: bfloat16 [2, 640, 2048], P('rep', 's')
- output 4: bfloat16 [2, 2048, 640], P('rep', 's')
All inputs are finite; a program needn't handle non-finite values.
Results may differ from a plain program's by a relative error of at most 0.018.
Values are sent between devices in bfloat16 or wider.
A program may use at most 2 GiB of HBM per device.

v0:
```python
import functools

import jax
import jax.numpy as jnp
from jax import lax
from jax.experimental import pallas as pl
from jax.experimental.pallas import tpu as pltpu
from jax.sharding import PartitionSpec as P

F32, BF16 = jnp.float32, jnp.bfloat16
MESH = pl.DeviceIdType.MESH
VMEM_LIMIT = 66_000_000
EPS = 1e-6


def dot(a, b, dims=((1,), (0,))):
    return lax.dot_general(a, b, (dims, ((), ())), preferred_element_type=F32)


def places():
    me = lax.axis_index("s")
    core, y, x = me % 2, (me // 2) % 2, me // 4
    to_x, to_y = 4 - 8 * x, 2 - 4 * y
    return me, me + 1 - 2 * core, me + to_x, me + to_y, me + to_x + to_y


def all_peers():
    _, mate, *near = places()
    z = lax.axis_index("r")
    return [{"s": p} for p in (mate, *near)] + [{"r": (z + k) % 4} for k in (1, 2, 3)]


def greet(peers):
    barrier = pltpu.get_barrier_semaphore()
    for peer in peers:
        pl.semaphore_signal(barrier, inc=1, device_id=peer, device_id_type=MESH)
    pl.semaphore_wait(barrier, len(peers))


def remote(src, dst, send, recv, peer):
    return pltpu.make_async_remote_copy(src_ref=src, dst_ref=dst, send_sem=send, recv_sem=recv, device_id=peer, device_id_type=MESH)


class Piece:
    def __init__(self, block, at, half, send, recv):
        self.me, self.mate, self.xn, self.yn, self.dn = places()
        self.block, self.at, self.half, self.send, self.recv = block, at, half, send, recv

    def copy(self, k):
        sems = self.send.at[k], self.recv.at[k]
        if k < 3:
            return remote(self.block, self.at(self.me), *sems, {"s": (self.mate, self.xn, self.yn)[k]})
        if k == 3:
            return remote(self.half(self.xn, 0), self.half(self.xn, 0), *sems, {"s": self.yn})
        if k == 4:
            return remote(self.half(self.yn, 1), self.half(self.yn, 1), *sems, {"s": self.xn})
        which = (self.xn, self.yn, self.dn)[k - 5]
        return remote(self.at(which), self.at(which), *sems, {"s": self.mate})

    def begin(self):
        for k in (1, 2, 0):
            self.copy(k).start()

    def forward(self):
        self.copy(1).wait_recv()
        self.copy(2).wait_recv()
        for k in (3, 4, 5, 6):
            self.copy(k).start()

    def relay(self):
        self.copy(3).wait_recv()
        self.copy(4).wait_recv()
        self.copy(7).start()

    def settle(self):
        for k in (0, 5, 6, 7):
            self.copy(k).wait_recv()

    def drain(self):
        for k in range(8):
            self.copy(k).wait_send()


def by_columns(block, whole, first, count, *sems):
    cut = lambda slot, start, n: whole.at[slot, :, pl.ds(start, n)]
    return Piece(
        block.at[0, :, pl.ds(first, count)],
        lambda slot: cut(slot, first, count),
        lambda slot, h: cut(slot, first + h * (count // 2), count // 2),
        *sems,
    )


def by_rows(block, whole, *sems):
    n = whole.shape[1] // 2
    return Piece(block.at[0], lambda slot: whole.at[slot], lambda slot, h: whole.at[slot, pl.ds(h * n, n), :], *sems)


def normed(h):
    wide = h.astype(F32)
    scale = lax.rsqrt(jnp.mean(wide * wide, -1, keepdims=True) + EPS)
    return wide, scale, (wide * scale).astype(BF16)


def forward_kernel(nt, nc, x, sg, su, sd, ng, nu, nd, out, og, ou, od, pg, pu, pd, wg, wu, wd, a, hidden, send, recv, local):
    step = pl.program_id(0)
    d, ff = wg.shape[0] * wg.shape[1], wg.shape[2]
    tile, chunk = x.shape[0], ff // nc
    me = lax.axis_index("s")
    sems = lambda n: (send.at[n], recv.at[n])
    c = [
        [by_columns(shard, whole, k * chunk, chunk, *sems(2 * k + n)) for n, (shard, whole) in enumerate([(sg, wg), (su, wu)])]
        for k in range(nc)
    ]
    down = [by_rows(sd, wd, *sems(2 * nc))]
    g1 = [by_columns(ng, pg, 0, ff, *sems(2 * nc + 1))]
    u1 = [by_columns(nu, pu, 0, ff, *sems(2 * nc + 2))]
    d1 = [by_rows(nd, pd, *sems(2 * nc + 3))]
    keep = [pltpu.make_async_copy(p.at[0], q.at[me], local.at[n]) for n, (p, q) in enumerate([(ng, pg), (nu, pu), (nd, pd)])]
    save = [pltpu.make_async_copy(p, q, local.at[3 + n]) for n, (p, q) in enumerate([(wg, og), (wu, ou), (wd, od)])]

    def do(*acts):
        for name, pieces in acts:
            for piece in pieces:
                getattr(piece, name)()

    def first():
        mate, xn, yn = places()[1:4]
        greet([{"s": p} for p in (mate, xn, yn)])
        do(("begin", c[0]), ("begin", c[1]))
        for shard, whole in ((sg, wg), (su, wu), (sd, wd)):
            whole[me] = shard[0]
        for copy in keep:
            copy.start()
        do(("forward", c[0]), ("begin", c[2]), ("relay", c[0]), ("settle", c[0]))

    def all_here():
        do(("settle", down))
        for copy in save:
            copy.start()

    plan = {
        0: first,
        1: lambda: do(("forward", c[1]), ("begin", c[3])),
        3: lambda: do(("relay", c[1]), ("forward", c[2]), ("begin", down)),
        4: lambda: do(("settle", c[1])),
        5: lambda: do(("forward", c[3]), ("begin", g1)),
        6: lambda: do(("relay", c[2])),
        8: lambda: do(("settle", c[2])),
        9: lambda: do(("forward", down), ("begin", u1)),
        10: lambda: do(("relay", c[3])),
        12: lambda: do(("settle", c[3])),
        13: lambda: do(("forward", g1), ("begin", d1)),
        14: lambda: do(("relay", down)),
        16: all_here,
        17: lambda: do(("forward", u1)),
        18: lambda: do(("relay", g1)),
    }
    for n, f in plan.items():
        pl.when(step == n)(f)

    @pl.when(step < nt)
    def _():
        a[step] = normed(x[...])[2]

    @pl.when(step < nt * nc)
    def _():
        cut = pl.ds(pl.multiple_of(step // nt * chunk, chunk), chunk)
        here = a[step % nt]
        gate = dot(here, wg[:, :, cut].reshape(d, chunk))
        up = dot(here, wu[:, :, cut].reshape(d, chunk))
        hidden[step % nt, :, cut] = (gate * lax.logistic(gate) * up).astype(BF16)

    @pl.when(step >= nt * nc)
    def _():
        below = dot(hidden[step - nt * nc], wd[...].reshape(ff, d)).astype(BF16)
        out[...] = (x[...].astype(F32) + below.astype(F32)).astype(BF16)

    @pl.when(step == nt * nc + nt - 1)
    def _():
        do(("forward", d1), ("relay", u1), ("relay", d1), ("settle", g1), ("settle", u1), ("settle", d1))
        for pieces in (*c, down, g1, u1, d1):
            do(("drain", pieces))
        for copy in (*keep, *save):
            copy.wait()


def constant(shape):
    return pl.BlockSpec(shape, lambda i: (0,) * len(shape), pipeline_mode=pl.Buffered(1))


def forward(x, shards, collective_id, nt=4, nc=4):
    tokens, d = x.shape
    ff = shards[0].shape[2]
    tile = tokens // nt
    wholes = [(8, *w.shape[1:]) for w in shards]
    spot = lambda i: jnp.where(i < nt, i, jnp.where(i < nt * nc, nt - 1, i - nt * nc))
    layer = lambda w, n: pl.BlockSpec((1, *w.shape[1:]), lambda i: (n, 0, 0), pipeline_mode=pl.Buffered(1))
    out, *got = pl.pallas_call(
        functools.partial(forward_kernel, nt, nc),
        grid=(nt * nc + nt,),
        out_shape=[jax.ShapeDtypeStruct(x.shape, BF16), *[jax.ShapeDtypeStruct(w, BF16) for w in wholes * 2]],
        in_specs=[pl.BlockSpec((tile, d), lambda i: (spot(i), 0)), *[layer(w, n) for n in range(2) for w in shards]],
        out_specs=[pl.BlockSpec((tile, d), lambda i: (jnp.maximum(i - nt * nc, 0), 0)), *[pl.BlockSpec(memory_space=pl.ANY)] * 6],
        scratch_shapes=[
            *[pltpu.VMEM(w, BF16) for w in wholes],
            pltpu.VMEM((nt, tile, d), BF16),
            pltpu.VMEM((nt, tile, ff), BF16),
            pltpu.SemaphoreType.DMA((2 * nc + 4, 8)),
            pltpu.SemaphoreType.DMA((2 * nc + 4, 8)),
            pltpu.SemaphoreType.DMA((6,)),
        ],
        compiler_params=pltpu.CompilerParams(
            collective_id=collective_id, has_side_effects=True, vmem_limit_bytes=VMEM_LIMIT, dimension_semantics=("arbitrary",)
        ),
        cost_estimate=pl.CostEstimate(flops=6 * tokens * d * ff, bytes_accessed=4 * tokens * d, transcendentals=0),
        name="forward",
    )(x, *shards, *shards)
    got = [w.reshape(-1, w.shape[-1]) for w in got]
    return out, [got[:3], got[3:]]


def act_kernel(steps, chunk, sums, h, dy, wg, wu, wd, *refs):
    step = pl.program_id(0)
    if sums:
        far_g, far_u, by_gu, a_t, by_down, out_g, out_u, total, *scratch, term_g, term_u, local = refs
        loads = [pltpu.make_async_copy(a, b, local.at[n]) for n, (a, b) in enumerate([(far_g, term_g), (far_u, term_u)])]
        gate_sum = Sum(1, term_g, *scratch[:6], scratch[-2:])
        up_sum = Sum(2, term_u, *scratch[6:12], scratch[-2:])

        def begin():
            for load in loads:
                load.start()
            greet(all_peers())
            gate_sum.pair(far_g)
            up_sum.pair(far_u)

        def second():
            for load in loads:
                load.wait()
            gate_sum.chips(far_g)
            up_sum.chips(far_u)

        plan = [(0, begin), (1, second), (3, gate_sum.groups), (4, gate_sum.share), (5, up_sum.groups), (6, up_sum.share)]
        for n, f in plan:
            pl.when(step == steps * n // 8)(f)
    else:
        by_gu, a_t, by_down, total = refs

    @pl.when(step == 0)
    def _():
        total[...] = jnp.zeros_like(total)

    _, _, a = normed(h[...])
    g = dy[...]
    a_t[...] = a.T
    g_t = g.T
    for j in range(wg.shape[1] // chunk):
        cut = pl.ds(j * chunk, chunk)
        gate, up = dot(a, wg[:, cut]), dot(a, wu[:, cut])
        by_hidden = dot(g, wd[cut, :], ((1,), (1,))).astype(BF16).astype(F32)
        share = lax.logistic(gate)
        silu = gate * share
        by_gu[0, :, cut] = (by_hidden * up * (share + silu * (1.0 - share))).astype(BF16)
        by_gu[1, :, cut] = (by_hidden * silu).astype(BF16)
        total[:, cut] += dot(g_t, (silu * up).astype(BF16))

    @pl.when(step == steps - 1)
    def _():
        n = by_down.shape[1]
        for s in range(by_down.shape[0]):
            by_down[s] = total[:, s * n : (s + 1) * n].T.astype(BF16)
        if sums:
            gate_sum.end(out_g)
            up_sum.end(out_u)


def act(h, dy, weights, terms=(), collective_id=None, tile=512, chunk=256):
    tokens, d = h.shape
    ff = weights[0].shape[1]
    steps = tokens // tile
    rows = pl.BlockSpec((tile, d), lambda i: (i, 0))
    block = (d // 8, ff)
    scratch, extra = [], {}
    if terms:
        scratch = [*sum_scratch(1, *block), *sum_scratch(2, *block), pltpu.SemaphoreType.DMA((3, 13)), pltpu.SemaphoreType.DMA((3, 13))]
        scratch += [pltpu.VMEM(w.shape, BF16) for w in terms] + [pltpu.SemaphoreType.DMA((2,))]
        extra = dict(collective_id=collective_id, has_side_effects=True)
    return pl.pallas_call(
        functools.partial(act_kernel, steps, chunk, bool(terms)),
        grid=(steps,),
        out_shape=[
            jax.ShapeDtypeStruct((2, tokens, ff), BF16),
            jax.ShapeDtypeStruct((d, tokens), BF16),
            jax.ShapeDtypeStruct((8, ff // 8, d), BF16),
            *[jax.ShapeDtypeStruct(block, BF16) for _ in terms],
        ],
        in_specs=[rows, rows, *[constant(w.shape) for w in weights], *[pl.BlockSpec(memory_space=pl.ANY) for _ in terms]],
        out_specs=[
            pl.BlockSpec((2, tile, ff), lambda i: (0, i, 0)),
            pl.BlockSpec((d, tile), lambda i: (0, i)),
            pl.BlockSpec((8, ff // 8, d), lambda i: (0, 0, 0)),
            *[pl.BlockSpec(block, lambda i: (0, 0)) for _ in terms],
        ],
        scratch_shapes=[pltpu.VMEM((d, ff), F32), *scratch],
        compiler_params=pltpu.CompilerParams(vmem_limit_bytes=VMEM_LIMIT, dimension_semantics=("arbitrary",), **extra),
        cost_estimate=pl.CostEstimate(flops=8 * tokens * d * ff, bytes_accessed=8 * tokens * ff, transcendentals=0),
        name="act",
    )(h, dy, *weights, *terms)


class Sum:
    def __init__(self, m, term, got0, got1, own, parts, got2, done, sems):
        self.m, self.term, self.got0, self.got1, self.own, self.parts, self.got2, self.done = m, term, got0, got1, own, parts, got2, done
        self.sems = sems
        self.me, self.mate, xn, yn, dn = places()
        self.near = (xn, yn, dn)
        self.z = lax.axis_index("r")
        self.core, self.chip = self.me % 2, self.me // 2

    def copy(self, k, term=None):
        sems = self.sems[0].at[self.m, k], self.sems[1].at[self.m, k]
        if k < 4:
            return remote((self.term if term is None else term).at[2 * k + 1 - self.core], self.got0.at[k], *sems, {"s": self.mate})
        if k < 7:
            to = self.near[k - 4]
            return remote(self.got0.at[to // 2], self.got1.at[k - 4], *sems, {"s": to})
        if k < 10:
            z = (self.z + k - 6) % 4
            return remote(self.parts.at[z], self.got2.at[k - 7], *sems, {"r": z})
        z = (self.z + k - 9) % 4
        return remote(self.done.at[self.z], self.done.at[self.z], *sems, {"r": z})

    def start(self, ks):
        for k in ks:
            self.copy(k).start()

    def wait(self, ks):
        for k in ks:
            self.copy(k).wait()

    def pair(self, term=None):
        for k in range(4):
            self.copy(k, term).start()

    def chips(self, term=None):
        for k in range(4):
            self.copy(k, term).wait()
        for k, to in enumerate(self.near):
            chip = to // 2
            self.got0[chip] = (self.term[2 * chip + self.core].astype(F32) + self.got0[chip].astype(F32)).astype(BF16)
            self.copy(4 + k).start()
        self.own[...] = self.term[self.me].astype(F32) + self.got0[self.chip].astype(F32)

    def groups(self):
        self.wait(range(4, 7))
        whole = self.own[...] + self.got1[0].astype(F32) + self.got1[1].astype(F32) + self.got1[2].astype(F32)
        self.own[...] = whole
        n = self.parts.shape
        for q in range(4):
            self.parts[q] = (whole[:, q * n[2] : (q + 1) * n[2]] if self.m else whole[q * n[1] : (q + 1) * n[1]]).astype(BF16)
        self.start(range(7, 10))

    def share(self):
        self.wait(range(7, 10))
        n = self.parts.shape
        if self.m:
            mine = self.own[:, pl.ds(pl.multiple_of(self.z * n[2], 128), n[2])]
        else:
            mine = self.own[pl.ds(pl.multiple_of(self.z * n[1], 8), n[1]), :]
        for k in range(3):
            mine = mine + self.got2[k].astype(F32)
        self.done[self.z] = mine.astype(BF16)
        self.start(range(10, 13))

    def end(self, out):
        self.wait(range(10, 13))
        n = self.parts.shape
        for q in range(4):
            if self.m:
                out[:, q * n[2] : (q + 1) * n[2]] = self.done[q]
            else:
                out[q * n[1] : (q + 1) * n[1], :] = self.done[q]


def sum_scratch(m, rows, cols):
    part = (4, rows, cols // 4) if m else (4, rows // 4, cols)
    return [
        pltpu.VMEM((4, rows, cols), BF16),
        pltpu.VMEM((3, rows, cols), BF16),
        pltpu.VMEM((rows, cols), F32),
        pltpu.VMEM(part, BF16),
        pltpu.VMEM((3, *part[1:]), BF16),
        pltpu.VMEM(part, BF16),
    ]


def tail_kernel(nw, nt, last, a_t, wide_gu, by_gu, h, dy, far_wg, far_wu, far_down, by_h, out_d, *refs):
    step = pl.program_id(0)
    end = 2 * nw + nt - 1
    *refs, wg, wu, by_down, local = refs
    loads = [pltpu.make_async_copy(a, b, local.at[n]) for n, (a, b) in enumerate([(far_down, by_down), (far_wg, wg), (far_wu, wu)])]
    if last:
        out_g, out_u, term_g, term_u, *scratch = refs
        gate, up = Sum(1, term_g, *scratch[6:12], scratch[-2:]), Sum(2, term_u, *scratch[12:18], scratch[-2:])
    else:
        term_g, term_u, *scratch = refs
    down = Sum(0, by_down, *scratch[0:6], scratch[-2:])

    def begin():
        for load in loads:
            load.start()
        greet(all_peers())
        down.pair(far_down)

    def second():
        loads[0].wait()
        down.chips(far_down)

    def third():
        loads[1].wait()
        loads[2].wait()

    plan = [(0, begin), (1, second), (2 * nw, third), (nw + nw // 2, down.groups), (2 * nw, down.share), (2 * nw + 3, lambda: down.end(out_d))]
    if last:
        plan += [(nw, gate.pair), (nw + 1, gate.chips), (2 * nw + nt // 4, gate.groups), (2 * nw + nt // 2, gate.share)]
        plan += [(2 * nw, up.pair), (2 * nw + 1, up.chips), (end - 1, up.groups)]
    for n, f in plan:
        pl.when(step == n)(f)

    def weight(term, n):
        width = wide_gu.shape[2]
        got = dot(a_t[...], wide_gu[0]).astype(BF16)
        rows = term.shape[1]
        for s in range(8):
            term[s, :, pl.ds(pl.multiple_of(n * width, 128), width)] = got[s * rows : (s + 1) * rows]

    @pl.when(step < nw)
    def _():
        weight(term_g, step)

    @pl.when((step >= nw) & (step < 2 * nw))
    def _():
        weight(term_u, step - nw)

    @pl.when(step >= 2 * nw)
    def _():
        by_a = (dot(wg[...], by_gu[0], ((1,), (1,))) + dot(wu[...], by_gu[1], ((1,), (1,)))).T
        by_a = by_a.astype(BF16).astype(F32)
        wide = h[...].astype(F32)
        scale = lax.rsqrt(jnp.mean(wide * wide, -1, keepdims=True) + EPS)
        pull = jnp.mean(by_a * wide, -1, keepdims=True) * scale * scale * scale
        by_h[...] = (dy[...].astype(F32) + (by_a * scale - wide * pull).astype(BF16).astype(F32)).astype(BF16)

    if last:

        @pl.when(step == end)
        def _():
            up.share()
            gate.end(out_g)
            up.end(out_u)


def tail(a_t, by_gu, wg, wu, h, dy, by_down, last_layer, collective_id, width=512, tile=512):
    d, tokens = a_t.shape
    ff = wg.shape[1]
    nw, nt = ff // width, tokens // tile
    place = lambda i: jnp.maximum(i - 2 * nw, 0)
    rows = pl.BlockSpec((tile, d), lambda i: (place(i), 0))
    last = 2 * nw - 1
    gate_block, down_block = (d // 8, ff), (ff // 8, d)
    whole = lambda shape: pl.BlockSpec(shape, lambda i: (0,) * len(shape))
    blocks = [gate_block] * 2 if last_layer else [(8, *gate_block)] * 2
    scratch = sum_scratch(0, *down_block)
    if last_layer:
        scratch = [pltpu.VMEM((8, *gate_block), BF16)] * 2 + scratch + sum_scratch(1, *gate_block) + sum_scratch(2, *gate_block)
    return pl.pallas_call(
        functools.partial(tail_kernel, nw, nt, last_layer),
        grid=(2 * nw + nt,),
        out_shape=[
            jax.ShapeDtypeStruct((tokens, d), BF16),
            jax.ShapeDtypeStruct(down_block, BF16),
            *[jax.ShapeDtypeStruct(b, BF16) for b in blocks],
        ],
        in_specs=[
            constant(a_t.shape),
            pl.BlockSpec((1, tokens, width), lambda i: (jnp.minimum(i, last) // nw, 0, jnp.minimum(i, last) % nw)),
            pl.BlockSpec((2, tile, ff), lambda i: (0, place(i), 0)),
            rows,
            rows,
            *[pl.BlockSpec(memory_space=pl.ANY)] * 3,
        ],
        out_specs=[
            rows,
            whole(down_block),
            *[whole(b) for b in blocks],
        ],
        scratch_shapes=[
            *scratch,
            pltpu.SemaphoreType.DMA((3, 13)),
            pltpu.SemaphoreType.DMA((3, 13)),
            *[pltpu.VMEM(w.shape, BF16) for w in (wg, wu, by_down)],
            pltpu.SemaphoreType.DMA((3,)),
        ],
        compiler_params=pltpu.CompilerParams(
            collective_id=collective_id, has_side_effects=True, vmem_limit_bytes=VMEM_LIMIT, dimension_semantics=("arbitrary",)
        ),
        cost_estimate=pl.CostEstimate(flops=8 * tokens * d * ff, bytes_accessed=8 * tokens * ff, transcendentals=0),
        name="tail",
    )(a_t, by_gu, by_gu, h, dy, wg, wu, by_down)


def solution(mesh):
    def step(x, dy, *shards):
        layers = shards[0].shape[0]
        assert layers == 2
        h, weights = forward(x[0], shards, 1)
        inputs = [x[0], h]
        by_h, mine, terms = dy[0], [None] * layers, ()
        for n in reversed(range(layers)):
            by_gu, a_t, by_down, *summed = act(inputs[n], by_h, weights[n], terms, 2 * layers + n)
            if terms:
                mine[n + 1] = [*summed, mine[n + 1]]
            by_h, by_d, *terms = tail(a_t, by_gu, *weights[n][:2], inputs[n], by_h, by_down, n == 0, layers + n)
            mine[n] = by_d if n else [*terms, by_d]
        return (by_h[None], *(jnp.stack([mine[n][i] for n in range(layers)]) for i in range(3)))

    states, cut = P(("rep", "r", "s"), None, None), P(None, "s", None)
    return jax.shard_map(
        step,
        mesh=mesh,
        in_specs=(states, states) + (cut,) * 3,
        out_specs=(states,) + (P("rep", "s", None),) * 3,
        check_vma=False,
    )
```

profile of v0, /device:TPU:0, one launch (start us, length us, event | category | flops | bytes accessed | tf_op | source)
XLA Modules:
  0.0 370.5 jit_solution(14697796222883058168)
XLA Ops:
  0.6 76.9 %forward.1 = (bf16[4096,640]{1,0:T(8,128)(2,1)}, bf16[8,80,2048]{2,1,0:T(8,128)(2,1)}, bf16[8,80,2048]{2,1,0:T(8,128)(2,1)}, bf16[8,256,640]{2,1,0:T(8,128)(2,1)...) custom-call(bf16[4096,640]{1,0:T(8,128)(2,1)} %bitcast.24, ...), custom_call_target="tpu_custom_call" | custom-call | flops 32212254720 | bytes 10485760 | tf_op jit(solution)/shard_map/forward/pallas_call | solution.py:199
  77.6 65.3 %act.2 = (bf16[2,4096,2048]{2,1,0:T(8,128)(2,1)}, bf16[640,4096]{1,0:T(8,128)(2,1)}, bf16[8,256,640]{2,1,0:T(8,128)(2,1)}) custom-call(bf16[4096,640]{1,0:T(8,128)(2,1)} %get-tuple-element.27.h, bf16[4096,640]{1,0:T(8,128)(2,1)} %bitcast.22, bf16[640,2048]{1,0:T(8,128)(2,1)} %bitcast.32, bf16[640,2048]{1,0:T(8,128)(2,1)} %bitcast.34, bf16[2048,640]{1,0:T(8,128)(2,1)} %bitcast.36), custom_call_target="tpu_custom_call" | custom-call | flops 42949672960 | bytes 67108864 | tf_op jit(solution)/shard_map/act/pallas_call | solution.py:289
  142.9 67.5 %tail.2 = (bf16[4096,640]{1,0:T(8,128)(2,1)}, bf16[256,640]{1,0:T(8,128)(2,1)}, bf16[8,80,2048]{2,1,0:T(8,128)(2,1)}, bf16[8,80,2048]{2,1,0:T(8,128)(2,1)}) custom-call(bf16[640,4096]{1,0:T(8,128)(2,1)} %get-tuple-element.31.a_t, bf16[2,4096,2048]{2,1,0:T(8,128)(2,1)} %get-tuple-element.32.wide_gu.by_gu, ...), custom_call_target="tpu_custom_call" | custom-call | flops 42949672960 | bytes 67108864 | tf_op jit(solution)/shard_map/tail/pallas_call | solution.py:477
  210.3 74.1 %act.3 = (bf16[2,4096,2048]{2,1,0:T(8,128)(2,1)}, bf16[640,4096]{1,0:T(8,128)(2,1)}, bf16[8,256,640]{2,1,0:T(8,128)(2,1)}, bf16[80,2048]{1,0:T(8,128)(2,1)}, bf16[80,2048]{1,0:T(8,128)(2,1)}) custom-call(bf16[4096,640]{1,0:T(8,128)(2,1)} %bitcast.25, bf16[4096,640]{1,0:T(8,128)(2,1)} %get-tuple-element.34.dy, bf16[640,2048]{1,0:T(8,128)(2,1)} %bitcast.27, ...), custom_call_target="tpu_custom_call" | custom-call | flops 42949672960 | bytes 67108864 | tf_op jit(solution)/shard_map/act/pallas_call | solution.py:289
  284.5 0.0 copy-start.1
  284.5 0.0 copy-start.2
  284.5 0.0 copy-start
  284.5 76.6 %tail.3 = (bf16[4096,640]{1,0:T(8,128)(2,1)}, bf16[256,640]{1,0:T(8,128)(2,1)}, bf16[80,2048]{1,0:T(8,128)(2,1)}, bf16[80,2048]{1,0:T(8,128)(2,1)}) custom-call(bf16[640,4096]{1,0:T(8,128)(2,1)} %get-tuple-element.40.a_t, bf16[2,4096,2048]{2,1,0:T(8,128)(2,1)} %get-tuple-element.41.wide_gu.by_gu, bf16[2,4096,2048]{2,1,0:T(8,128)(2,1)} %get-tuple-element.41.wide_gu.by_gu, ...), custom_call_target="tpu_custom_call" | custom-call | flops 42949672960 | bytes 67108864 | tf_op jit(solution)/shard_map/tail/pallas_call | solution.py:477
  361.1 0.0 copy-done.1
  361.1 0.0 copy-done.2
  361.1 2.2 pad_maximum_fusion
  363.4 0.0 copy-done
  363.4 1.9 pad_maximum_fusion.2
  365.2 5.3 %copy.10 = bf16[1,4096,640]{2,1,0:T(8,128)(2,1)} copy(bf16[1,4096,640]{2,1,0:T(8,128)(2,1)} %bitcast.15) | data formatting | bytes 10485760
Async XLA Ops:
  284.5 76.6 %copy-start.1 = (bf16[80,2048]{1,0:T(8,128)(2,1)S(1)}, bf16[80,2048]{1,0:T(8,128)(2,1)}, u32[]{:S(2)}) copy-start(bf16[80,2048]{1,0:T(8,128)(2,1)} %get-tuple-element.45) | copy-start | bytes 983044
  284.5 76.6 %copy-start.2 = (bf16[80,2048]{1,0:T(8,128)(2,1)S(1)}, bf16[80,2048]{1,0:T(8,128)(2,1)}, u32[]{:S(2)}) copy-start(bf16[80,2048]{1,0:T(8,128)(2,1)} %get-tuple-element.47) | copy-start | bytes 983044
  284.5 78.9 %copy-start = (bf16[256,640]{1,0:T(8,128)(2,1)S(1)}, bf16[256,640]{1,0:T(8,128)(2,1)}, u32[]{:S(2)}) copy-start(bf16[256,640]{1,0:T(8,128)(2,1)} %get-tuple-element.49) | copy-start | bytes 983044
where the time goes:
time: 371 us
  Pallas kernels  360 us (97%)
  local copies, waits for them, and re-layouts  5.3 us (1%)
  other arithmetic  4.12 us (1%)
    pallas_call x2, Pallas kernels, tail(): pl.pallas_call(functools.partial(tail_kernel, nw, nt, last_layer), grid=(...  144 us
    pallas_call x2, Pallas kernels, act(): pl.pallas_call(functools.partial(act_kernel, steps, chunk, bool(terms)),...  139 us
    pallas_call x1, Pallas kernels, forward(): pl.pallas_call(functools.partial(forward_kernel, nt, nc), grid=(nt * nc +...  76.9 us

commit v1 on v0

--- a/solution.py
+++ b/solution.py
@@ -30,11 +30,19 @@
     return [{"s": p} for p in (mate, *near)] + [{"r": (z + k) % 4} for k in (1, 2, 3)]
 
 
-def greet(peers):
+def hail(peers):
     barrier = pltpu.get_barrier_semaphore()
     for peer in peers:
         pl.semaphore_signal(barrier, inc=1, device_id=peer, device_id_type=MESH)
-    pl.semaphore_wait(barrier, len(peers))
+
+
+def hear(peers):
+    pl.semaphore_wait(pltpu.get_barrier_semaphore(), len(peers))
+
+
+def greet(peers):
+    hail(peers)
+    hear(peers)
 
 
 def remote(src, dst, send, recv, peer):
@@ -146,15 +154,12 @@
         4: lambda: do(("settle", c[1])),
         5: lambda: do(("forward", c[3]), ("begin", g1)),
         6: lambda: do(("relay", c[2])),
-        8: lambda: do(("settle", c[2])),
-        9: lambda: do(("forward", down), ("begin", u1)),
-        10: lambda: do(("relay", c[3])),
-        12: lambda: do(("settle", c[3])),
-        13: lambda: do(("forward", g1), ("begin", d1)),
-        14: lambda: do(("relay", down)),
+        8: lambda: do(("settle", c[2]), ("forward", down), ("begin", u1)),
+        9: lambda: do(("relay", c[3])),
+        12: lambda: do(("settle", c[3]), ("relay", down), ("forward", g1), ("begin", d1)),
         16: all_here,
-        17: lambda: do(("forward", u1)),
-        18: lambda: do(("relay", g1)),
+        17: lambda: do(("forward", u1), ("relay", g1)),
+        19: lambda: do(("forward", d1)),
     }
     for n, f in plan.items():
         pl.when(step == n)(f)
@@ -178,7 +183,7 @@
 
     @pl.when(step == nt * nc + nt - 1)
     def _():
-        do(("forward", d1), ("relay", u1), ("relay", d1), ("settle", g1), ("settle", u1), ("settle", d1))
+        do(("relay", u1), ("relay", d1), ("settle", g1), ("settle", u1), ("settle", d1))
         for pieces in (*c, down, g1, u1, d1):
             do(("drain", pieces))
         for copy in (*keep, *save):
@@ -241,7 +246,7 @@
             gate_sum.chips(far_g)
             up_sum.chips(far_u)
 
-        plan = [(0, begin), (1, second), (3, gate_sum.groups), (4, gate_sum.share), (5, up_sum.groups), (6, up_sum.share)]
+        plan = [(0, begin), (1, second), (3, gate_sum.groups), (5, gate_sum.share), (5, up_sum.groups), (7, up_sum.share)]
         for n, f in plan:
             pl.when(step == steps * n // 8)(f)
     else:
@@ -410,7 +415,10 @@
     def begin():
         for load in loads:
             load.start()
-        greet(all_peers())
+        hail(all_peers())
+
+    def meet():
+        hear(all_peers())
         down.pair(far_down)
 
     def second():
@@ -421,9 +429,10 @@
         loads[1].wait()
         loads[2].wait()
 
-    plan = [(0, begin), (1, second), (2 * nw, third), (nw + nw // 2, down.groups), (2 * nw, down.share), (2 * nw + 3, lambda: down.end(out_d))]
+    plan = [(0, begin), (1, meet), (2, second), (2 * nw, third)]
+    plan += [(2 * nw - 1, down.groups), (2 * nw + 1, down.share), (end - 3, lambda: down.end(out_d))]
     if last:
-        plan += [(nw, gate.pair), (nw + 1, gate.chips), (2 * nw + nt // 4, gate.groups), (2 * nw + nt // 2, gate.share)]
+        plan += [(nw, gate.pair), (nw + 1, gate.chips), (2 * nw + 2, gate.groups), (2 * nw + 4, gate.share)]
         plan += [(2 * nw, up.pair), (2 * nw + 1, up.chips), (end - 1, up.groups)]
     for n, f in plan:
         pl.when(step == n)(f)

time: 371 us -> 367 us (0.989)
  no operation moved by 1% of the time
where the time goes in v1:
time: 367 us
  Pallas kernels  357 us (97%)
  local copies, waits for them, and re-layouts  5.3 us (1%)
  other arithmetic  4.12 us (1%)
    pallas_call x2, Pallas kernels, tail(): pl.pallas_call(functools.partial(tail_kernel, nw, nt, last_layer), grid=(...  142 us
    pallas_call x2, Pallas kernels, act(): pl.pallas_call(functools.partial(act_kernel, steps, chunk, bool(terms)),...  138 us
    pallas_call x1, Pallas kernels, forward(): pl.pallas_call(functools.partial(forward_kernel, nt, nc), grid=(nt * nc +...  77.6 us

profile of v1, /device:TPU:0, one launch (start us, length us, event | category | flops | bytes accessed | tf_op | source)
XLA Modules:
  0.0 367.0 jit_solution(753796505509207969)
XLA Ops:
  0.6 77.6 %forward.1 = (bf16[4096,640]{1,0:T(8,128)(2,1)}, bf16[8,80,2048]{2,1,0:T(8,128)(2,1)}, bf16[8,80,2048]{2,1,0:T(8,128)(2,1)}, bf16[8,256,640]{2,1,0:T(8,128)(2,1)...) custom-call(bf16[4096,640]{1,0:T(8,128)(2,1)} %bitcast.24, ...), custom_call_target="tpu_custom_call" | custom-call | flops 32212254720 | bytes 10485760 | tf_op jit(solution)/shard_map/forward/pallas_call | solution.py:204
  78.3 65.3 %act.2 = (bf16[2,4096,2048]{2,1,0:T(8,128)(2,1)}, bf16[640,4096]{1,0:T(8,128)(2,1)}, bf16[8,256,640]{2,1,0:T(8,128)(2,1)}) custom-call(bf16[4096,640]{1,0:T(8,128)(2,1)} %get-tuple-element.27.h, bf16[4096,640]{1,0:T(8,128)(2,1)} %bitcast.22, bf16[640,2048]{1,0:T(8,128)(2,1)} %bitcast.32, bf16[640,2048]{1,0:T(8,128)(2,1)} %bitcast.34, bf16[2048,640]{1,0:T(8,128)(2,1)} %bitcast.36), custom_call_target="tpu_custom_call" | custom-call | flops 42949672960 | bytes 67108864 | tf_op jit(solution)/shard_map/act/pallas_call | solution.py:294
  143.5 66.0 %tail.2 = (bf16[4096,640]{1,0:T(8,128)(2,1)}, bf16[256,640]{1,0:T(8,128)(2,1)}, bf16[8,80,2048]{2,1,0:T(8,128)(2,1)}, bf16[8,80,2048]{2,1,0:T(8,128)(2,1)}) custom-call(bf16[640,4096]{1,0:T(8,128)(2,1)} %get-tuple-element.31.a_t, bf16[2,4096,2048]{2,1,0:T(8,128)(2,1)} %get-tuple-element.32.wide_gu.by_gu, ...), custom_call_target="tpu_custom_call" | custom-call | flops 42949672960 | bytes 67108864 | tf_op jit(solution)/shard_map/tail/pallas_call | solution.py:486
  209.6 72.3 %act.3 = (bf16[2,4096,2048]{2,1,0:T(8,128)(2,1)}, bf16[640,4096]{1,0:T(8,128)(2,1)}, bf16[8,256,640]{2,1,0:T(8,128)(2,1)}, bf16[80,2048]{1,0:T(8,128)(2,1)}, bf16[80,2048]{1,0:T(8,128)(2,1)}) custom-call(bf16[4096,640]{1,0:T(8,128)(2,1)} %bitcast.25, bf16[4096,640]{1,0:T(8,128)(2,1)} %get-tuple-element.34.dy, bf16[640,2048]{1,0:T(8,128)(2,1)} %bitcast.27, ...), custom_call_target="tpu_custom_call" | custom-call | flops 42949672960 | bytes 67108864 | tf_op jit(solution)/shard_map/act/pallas_call | solution.py:294
  281.9 0.0 copy-start.1
  281.9 0.0 copy-start.2
  281.9 0.0 copy-start
  281.9 75.6 %tail.3 = (bf16[4096,640]{1,0:T(8,128)(2,1)}, bf16[256,640]{1,0:T(8,128)(2,1)}, bf16[80,2048]{1,0:T(8,128)(2,1)}, bf16[80,2048]{1,0:T(8,128)(2,1)}) custom-call(bf16[640,4096]{1,0:T(8,128)(2,1)} %get-tuple-element.40.a_t, bf16[2,4096,2048]{2,1,0:T(8,128)(2,1)} %get-tuple-element.41.wide_gu.by_gu, bf16[2,4096,2048]{2,1,0:T(8,128)(2,1)} %get-tuple-element.41.wide_gu.by_gu, ...), custom_call_target="tpu_custom_call" | custom-call | flops 42949672960 | bytes 67108864 | tf_op jit(solution)/shard_map/tail/pallas_call | solution.py:486
  357.5 0.0 copy-done.1
  357.5 0.0 copy-done.2
  357.5 2.2 pad_maximum_fusion
  359.8 0.0 copy-done
  359.8 1.9 pad_maximum_fusion.2
  361.7 5.3 %copy.10 = bf16[1,4096,640]{2,1,0:T(8,128)(2,1)} copy(bf16[1,4096,640]{2,1,0:T(8,128)(2,1)} %bitcast.15) | data formatting | bytes 10485760
Async XLA Ops:
  281.9 75.6 %copy-start.1 = (bf16[80,2048]{1,0:T(8,128)(2,1)S(1)}, bf16[80,2048]{1,0:T(8,128)(2,1)}, u32[]{:S(2)}) copy-start(bf16[80,2048]{1,0:T(8,128)(2,1)} %get-tuple-element.45) | copy-start | bytes 983044
  281.9 75.6 %copy-start.2 = (bf16[80,2048]{1,0:T(8,128)(2,1)S(1)}, bf16[80,2048]{1,0:T(8,128)(2,1)}, u32[]{:S(2)}) copy-start(bf16[80,2048]{1,0:T(8,128)(2,1)} %get-tuple-element.47) | copy-start | bytes 983044
  281.9 77.9 %copy-start = (bf16[256,640]{1,0:T(8,128)(2,1)S(1)}, bf16[256,640]{1,0:T(8,128)(2,1)}, u32[]{:S(2)}) copy-start(bf16[256,640]{1,0:T(8,128)(2,1)} %get-tuple-element.49) | copy-start | bytes 983044
